TPU v7x, 32 devices: a whole 2x2x4 slice. The times are simulated.
32 devices in a mesh: row: 16 (over z, y, core), col: 2 (over x).
Axes of the slice: x: 2, y: 2, z: 4, core: 2. Of those that a mesh axis runs over, the one named last changes fastest.
Arguments:
- start: float32 [32768, 128], P(('row', 'col')), may hold values from -18 to 18
- couplings: bfloat16 [128, 5, 256, 256], P(('row', 'col')), may hold values from -0.15625 to 0.15625
- tile_cols: int32 [128, 5], P(('row', 'col')), may hold values from 0 to 19
- stiffness: float32 [32768], P(('row', 'col')), may hold values from 1.5 to 4
- masses: float32 [32768], P(('row', 'col')), may hold values from 0.8 to 2.5, as said below
- bounds: float32 [2], replicated, may hold values from 1.8 to 6.5, as said below
Outputs:
- basis: float32 [32768, 128], P(('row', 'col'))
- ritz: float32 [128, 128], replicated
Inputs may be any that keep to these rules, and one draw needn't show every extreme that they name: Positive masses. bounds[0] < bounds[1].
All inputs are finite; a program needn't handle non-finite values.
Results may differ from a plain program's by a relative error of at most 0.0014.
Values may be sent and summed in bfloat16 or wider, within the bound.
No kernel may reach another device: no remote copies, remote signals or barrier semaphores. Data moves between devices by JAX's collectives and lax.ppermute only.
A program may use at most 64 MiB of HBM per device.

v0:
```python
import jax
import jax.numpy as jnp
from jax import lax
from jax.sharding import PartitionSpec as P

DEGREE = 8


def with_halo(cells, sides, width):
    for axis, dim in sides:
        count = lax.axis_size(axis)
        ends = count - 1
        head = lax.slice_in_dim(cells, 0, width, axis=dim)
        tail = lax.slice_in_dim(cells, cells.shape[dim] - width, cells.shape[dim], axis=dim)
        cells = jnp.concatenate(
            [
                lax.ppermute(tail, axis, [(i, (i + 1) % count) for i in range(ends)]),
                cells,
                lax.ppermute(head, axis, [((i + 1) % count, i) for i in range(ends)]),
            ],
            axis=dim,
        )
    return cells


def matmul_high(left, right):
    return jnp.dot(left, right, precision=lax.Precision.HIGHEST, preferred_element_type=jnp.float32)


def cholesky_inverse(gram, identity):
    factor = jnp.linalg.cholesky(gram)
    return lax.linalg.triangular_solve(factor, identity, left_side=True, lower=True)


def per_device(start, couplings, tile_cols, stiffness, masses, bounds):
    rows_dev, vec_width = start.shape
    per_block = couplings.shape[0]
    tile_size = couplings.shape[2]
    node_count = rows_dev * lax.axis_size("row") * lax.axis_size("col")

    def coupled(vectors):
        rounded = vectors.astype(jnp.bfloat16)
        line = lax.all_gather(rounded[None], "col", axis=0, tiled=True)
        column_pad = with_halo(rounded[None], (("row", 0),), 1)
        here = lax.axis_index("col")
        count = lax.axis_size("col")
        left = lax.dynamic_index_in_dim(line, jnp.maximum(here - 1, 0), 0, keepdims=False)
        right = lax.dynamic_index_in_dim(line, jnp.minimum(here + 1, count - 1), 0, keepdims=False)
        left = jnp.where(here > 0, left, jnp.zeros_like(left))
        right = jnp.where(here < count - 1, right, jnp.zeros_like(right))
        sides = [rounded, column_pad[0], column_pad[2], left, right]
        stack = jnp.stack(sides).reshape(5 * per_block, tile_size, vec_width)
        picked = stack[tile_cols]
        products = jnp.einsum(
            "psab,psbk->pak", couplings, picked, preferred_element_type=jnp.float32
        )
        return products.reshape(rows_dev, vec_width)

    stiff_column = stiffness[:, None]
    inverse_mass = 1.0 / masses[:, None]

    def stiff(vectors):
        return stiff_column * vectors - coupled(vectors)

    cut_low = bounds[0]
    cut_high = bounds[1]
    center = 0.5 * (cut_high + cut_low)
    radius = 0.5 * (cut_high - cut_low)
    scale_first = -radius / center
    twice_inverse = 2.0 / scale_first
    previous = start
    current = scale_first / radius * (stiff(start) * inverse_mass - center * start)
    scale_now = scale_first
    for iteration in range(DEGREE - 1):
        scale_next = 1.0 / (twice_inverse - scale_now)
        following = (
            2.0 * scale_next / radius * (stiff(current) * inverse_mass - center * current)
            - scale_now * scale_next * previous
        )
        previous, current, scale_now = (current, following, scale_next)
    weighted = masses[:, None] / node_count
    identity = jnp.eye(vec_width, dtype=jnp.float32)
    gram_local = matmul_high(current.T, weighted * current)
    gram = lax.psum(gram_local, ("row", "col"))
    projected = lax.psum(matmul_high(current.T, stiff(current) / node_count), ("row", "col"))
    inverse = cholesky_inverse(gram, identity)
    basis = matmul_high(current, inverse.T)
    ritz = matmul_high(matmul_high(inverse, projected), inverse.T)
    return (basis, ritz)


def solution(mesh):
    return jax.shard_map(
        per_device,
        mesh=mesh,
        in_specs=(
            P(("row", "col"), None),
            P(("row", "col"), None, None, None),
            P(("row", "col"), None),
            P(("row", "col")),
            P(("row", "col")),
            P(),
        ),
        out_specs=(P(("row", "col"), None), P()),
        check_vma=False,
    )
```

profile of v0, /device:TPU:0, one launch (start us, length us, event | category | flops | bytes accessed | tf_op | source)
XLA Modules:
  0.0 429.3 jit_solution(4073234901786170040)
XLA Ops:
  18.3 8.2 %all-gather = bf16[2048,128]{1,0:T(8,128)(2,1)S(1)} all-gather(bf16[1024,128]{1,0:T(8,128)(2,1)S(1)} %get-tuple-element.17), channel_id=2, replica_groups=mesh['row'=16,'col'=2] {'col'}, dimensions={0}, use_global_device_ids=true | all-gather | bytes 786432 | tf_op jit(solution)/shard_map/all_gather | solution.py:43
  29.5 3.2 gather_fusion
  40.0 4.4 %collective-permute-start.2 = (bf16[1,1024,128]{2,1,0:T(8,128)(2,1)S(1)}, bf16[1,1024,128]{2,1,0:T(8,128)(2,1)}, u32[]{:S(2)}, u32[]{:S(2)}) collective-permute-start(bf16[1,1024,128]{2,1,0:T(8,128)(2,1)S(1)} %bitcast.273), channel_id=1, source_target_pairs={{0,2},{2,4},{4,6},{6,8},{8,10},{10,12},{12,14},{14,16},{16,18},{18... | collective-permute-start | bytes 786440 | tf_op jit(solution)/shard_map/ppermute | solution.py:17
  45.8 7.2 %all-gather.1 = bf16[2048,128]{1,0:T(8,128)(2,1)S(1)} all-gather(bf16[1024,128]{1,0:T(8,128)(2,1)S(1)} %get-tuple-element.23), channel_id=3, replica_groups=mesh['row'=16,'col'=2] {'col'}, dimensions={0}, use_global_device_ids=true | all-gather | bytes 786432 | tf_op jit(solution)/shard_map/all_gather | solution.py:43
  57.9 3.2 gather_fusion.1
  68.7 5.1 %collective-permute-start.4 = (bf16[1,1024,128]{2,1,0:T(8,128)(2,1)S(1)}, bf16[1,1024,128]{2,1,0:T(8,128)(2,1)}, u32[]{:S(2)}, u32[]{:S(2)}) collective-permute-start(bf16[1,1024,128]{2,1,0:T(8,128)(2,1)S(1)} %bitcast.269), channel_id=1, source_target_pairs={{0,2},{2,4},{4,6},{6,8},{8,10},{10,12},{12,14},{14,16},{16,18},{18... | collective-permute-start | bytes 786440 | tf_op jit(solution)/shard_map/ppermute | solution.py:17
  75.2 7.0 %all-gather.2 = bf16[2048,128]{1,0:T(8,128)(2,1)S(1)} all-gather(bf16[1024,128]{1,0:T(8,128)(2,1)S(1)} %get-tuple-element.15), channel_id=4, replica_groups=mesh['row'=16,'col'=2] {'col'}, dimensions={0}, use_global_device_ids=true | all-gather | bytes 786432 | tf_op jit(solution)/shard_map/all_gather | solution.py:43
  87.2 3.2 gather_fusion.2
  98.1 5.2 %collective-permute-start.6 = (bf16[1,1024,128]{2,1,0:T(8,128)(2,1)S(1)}, bf16[1,1024,128]{2,1,0:T(8,128)(2,1)S(1)}, u32[]{:S(2)}, u32[]{:S(2)}) collective-permute-start(bf16[1,1024,128]{2,1,0:T(8,128)(2,1)S(1)} %bitcast.275), channel_id=1, source_target_pairs={{0,2},{2,4},{4,6},{6,8},{8,10},{10,12},{12,14},{14,16},{16,18},{18... | collective-permute-start | bytes 786440 | tf_op jit(solution)/shard_map/ppermute | solution.py:17
  104.7 7.0 %all-gather.3 = bf16[2048,128]{1,0:T(8,128)(2,1)S(1)} all-gather(bf16[1024,128]{1,0:T(8,128)(2,1)S(1)} %get-tuple-element.13), channel_id=5, replica_groups=mesh['row'=16,'col'=2] {'col'}, dimensions={0}, use_global_device_ids=true | all-gather | bytes 786432 | tf_op jit(solution)/shard_map/all_gather | solution.py:43
  125.6 6.0 %collective-permute-start.8 = (bf16[1,1024,128]{2,1,0:T(8,128)(2,1)S(1)}, bf16[1,1024,128]{2,1,0:T(8,128)(2,1)S(1)}, u32[]{:S(2)}, u32[]{:S(2)}) collective-permute-start(bf16[1,1024,128]{2,1,0:T(8,128)(2,1)S(1)} %bitcast.277), channel_id=1, source_target_pairs={{0,2},{2,4},{4,6},{6,8},{8,10},{10,12},{12,14},{14,16},{16,18},{18... | collective-permute-start | bytes 786440 | tf_op jit(solution)/shard_map/ppermute | solution.py:17
  133.0 7.0 %all-gather.4 = bf16[2048,128]{1,0:T(8,128)(2,1)S(1)} all-gather(bf16[1024,128]{1,0:T(8,128)(2,1)S(1)} %get-tuple-element.11), channel_id=6, replica_groups=mesh['row'=16,'col'=2] {'col'}, dimensions={0}, use_global_device_ids=true | all-gather | bytes 786432 | tf_op jit(solution)/shard_map/all_gather | solution.py:43
  151.9 6.7 %collective-permute-start.10 = (bf16[1,1024,128]{2,1,0:T(8,128)(2,1)S(1)}, bf16[1,1024,128]{2,1,0:T(8,128)(2,1)}, u32[]{:S(2)}, u32[]{:S(2)}) collective-permute-start(bf16[1,1024,128]{2,1,0:T(8,128)(2,1)S(1)} %bitcast.279), channel_id=1, source_target_pairs={{0,2},{2,4},{4,6},{6,8},{8,10},{10,12},{12,14},{14,16},{16,18},{18... | collective-permute-start | bytes 786440 | tf_op jit(solution)/shard_map/ppermute | solution.py:17
  160.0 7.0 %all-gather.5 = bf16[2048,128]{1,0:T(8,128)(2,1)S(1)} all-gather(bf16[1024,128]{1,0:T(8,128)(2,1)S(1)} %get-tuple-element.9), channel_id=7, replica_groups=mesh['row'=16,'col'=2] {'col'}, dimensions={0}, use_global_device_ids=true | all-gather | bytes 786432 | tf_op jit(solution)/shard_map/all_gather | solution.py:43
  182.8 6.0 %collective-permute-start.12 = (bf16[1,1024,128]{2,1,0:T(8,128)(2,1)S(1)}, bf16[1,1024,128]{2,1,0:T(8,128)(2,1)}, u32[]{:S(2)}, u32[]{:S(2)}) collective-permute-start(bf16[1,1024,128]{2,1,0:T(8,128)(2,1)S(1)} %bitcast.281), channel_id=1, source_target_pairs={{0,2},{2,4},{4,6},{6,8},{8,10},{10,12},{12,14},{14,16},{16,18},{18... | collective-permute-start | bytes 786440 | tf_op jit(solution)/shard_map/ppermute | solution.py:17
  190.2 7.2 %all-gather.6 = bf16[2048,128]{1,0:T(8,128)(2,1)S(1)} all-gather(bf16[1024,128]{1,0:T(8,128)(2,1)S(1)} %get-tuple-element.7), channel_id=8, replica_groups=mesh['row'=16,'col'=2] {'col'}, dimensions={0}, use_global_device_ids=true | all-gather | bytes 786432 | tf_op jit(solution)/shard_map/all_gather | solution.py:43
  212.9 5.3 %collective-permute-start.14 = (bf16[1,1024,128]{2,1,0:T(8,128)(2,1)S(1)}, bf16[1,1024,128]{2,1,0:T(8,128)(2,1)S(1)}, u32[]{:S(2)}, u32[]{:S(2)}) collective-permute-start(bf16[1,1024,128]{2,1,0:T(8,128)(2,1)S(1)} %bitcast.267), channel_id=1, source_target_pairs={{0,2},{2,4},{4,6},{6,8},{8,10},{10,12},{12,14},{14,16},{16,18},{18... | collective-permute-start | bytes 786440 | tf_op jit(solution)/shard_map/ppermute | solution.py:17
  219.6 7.0 %all-gather.7 = bf16[2048,128]{1,0:T(8,128)(2,1)S(1)} all-gather(bf16[1024,128]{1,0:T(8,128)(2,1)S(1)} %get-tuple-element.30), channel_id=9, replica_groups=mesh['row'=16,'col'=2] {'col'}, dimensions={0}, use_global_device_ids=true | all-gather | bytes 786432 | tf_op jit(solution)/shard_map/all_gather | solution.py:43
  229.6 3.2 gather_fusion.7
  238.0 5.2 %collective-permute-start.16 = (bf16[1,1024,128]{2,1,0:T(8,128)(2,1)S(1)}, bf16[1,1024,128]{2,1,0:T(8,128)(2,1)S(1)}, u32[]{:S(2)}, u32[]{:S(2)}) collective-permute-start(bf16[1,1024,128]{2,1,0:T(8,128)(2,1)S(1)} %bitcast.265), channel_id=1, source_target_pairs={{0,2},{2,4},{4,6},{6,8},{8,10},{10,12},{12,14},{14,16},{16,18},{18... | collective-permute-start | bytes 786440 | tf_op jit(solution)/shard_map/ppermute | solution.py:17
  246.3 7.0 %all-gather.8 = bf16[2048,128]{1,0:T(8,128)(2,1)S(1)} all-gather(bf16[1024,128]{1,0:T(8,128)(2,1)S(1)} %get-tuple-element.5), channel_id=10, replica_groups=mesh['row'=16,'col'=2] {'col'}, dimensions={0}, use_global_device_ids=true | all-gather | bytes 786432 | tf_op jit(solution)/shard_map/all_gather | solution.py:43
  265.9 129.1 %all-reduce.3.cloned.1.call-done = (f32[128,128]{0,1:T(8,128)}, f32[128,128]{1,0:T(8,128)}) async-done(((f32[128,128]{0,1:T(8,128)}, f32[128,128]{1,0:T(8,128)}), (f32[128,128]{0,1:T(8,128)}, f32[128,128]{1,0:T(8,128)})) %all-reduce.3.cloned.1.call-update) | async-done | bytes 131088 | tf_op jit(solution)/shard_map/psum | solution.py:84
  396.9 11.7 %cholesky.17 = f32[128,128]{1,0:T(8,128)S(1)} custom-call(f32[128,128]{1,0:T(8,128)S(1)} %fusion.38), custom_call_target="Cholesky" | custom-call | tf_op jit(solution)/shard_map/jit(cholesky)/cholesky | solution.py:31
  409.9 9.8 %custom-call.6 = f32[1,128,128]{1,2,0:T(8,128)S(1)} custom-call(f32[1,128,128]{2,1,0:T(8,128)S(1)} %fusion.35), custom_call_target="InvertDiagBlocksLowerTriangular" | custom-call | tf_op jit(solution)/shard_map/triangular_solve | solution.py:32
  (129 shorter events, 139.6 us)
Async XLA Ops:
  7.2 25.6 %copy-start = (bf16[4,5,256,256]{3,2,1,0:T(8,128)(2,1)S(1)}, bf16[4,5,256,256]{3,2,1,0:T(8,128)(2,1)}, u32[]{:S(2)}) copy-start(bf16[4,5,256,256]{3,2,1,0:T(8,128)(2,1)} %param.7) | copy-start | bytes 7864324
  7.2 387.9 %all-reduce.3.cloned.1.call-start = ((), (), s32[]{:S(2)}) async-start(), calls=%async_computation | async-start | bytes 262144 | tf_op jit(solution)/shard_map/psum | solution.py:84
  9.2 17.4 %collective-permute-start = (bf16[1,1024,128]{2,1,0:T(8,128)(2,1)S(1)}, bf16[1,1024,128]{2,1,0:T(8,128)(2,1)S(1)}, u32[]{:S(2)}, u32[]{:S(2)}) collective-permute-start(bf16[1,1024,128]{2,1,0:T(8,128)(2,1)S(1)} %bitcast.271), channel_id=1, source_target_pairs={{0,2},{2,4},{4,6},{6,8},{8,10},{10,12},{12,14},{14,16},{16,18},{18... | collective-permute-start | bytes 786440 | tf_op jit(solution)/shard_map/ppermute | solution.py:17
  11.6 15.7 %collective-permute-start.1 = (bf16[1,1024,128]{2,1,0:T(8,128)(2,1)S(1)}, bf16[1,1024,128]{2,1,0:T(8,128)(2,1)S(1)}, u32[]{:S(2)}, u32[]{:S(2)}) collective-permute-start(bf16[1,1024,128]{2,1,0:T(8,128)(2,1)S(1)} %bitcast.272), channel_id=1, source_target_pairs={{2,0},{4,2},{6,4},{8,6},{10,8},{12,10},{14,12},{16,14},{18,16},{20... | collective-permute-start | bytes 786440 | tf_op jit(solution)/shard_map/ppermute | solution.py:19
  32.7 5.2 %copy-start.5 = (f32[1024]{0:T(1024)S(1)}, f32[1024]{0:T(1024)}, u32[]{:S(2)}) copy-start(f32[1024]{0:T(1024)} %param.9) | copy-start | bytes 12292
  40.0 13.0 %collective-permute-start.2 = (bf16[1,1024,128]{2,1,0:T(8,128)(2,1)S(1)}, bf16[1,1024,128]{2,1,0:T(8,128)(2,1)}, u32[]{:S(2)}, u32[]{:S(2)}) collective-permute-start(bf16[1,1024,128]{2,1,0:T(8,128)(2,1)S(1)} %bitcast.273), channel_id=1, source_target_pairs={{0,2},{2,4},{4,6},{6,8},{8,10},{10,12},{12,14},{14,16},{16,18},{18... | collective-permute-start | bytes 786440 | tf_op jit(solution)/shard_map/ppermute | solution.py:17
  44.4 10.3 %collective-permute-start.3 = (bf16[1,1024,128]{2,1,0:T(8,128)(2,1)S(1)}, bf16[1,1024,128]{2,1,0:T(8,128)(2,1)}, u32[]{:S(2)}, u32[]{:S(2)}) collective-permute-start(bf16[1,1024,128]{2,1,0:T(8,128)(2,1)S(1)} %bitcast.274), channel_id=1, source_target_pairs={{2,0},{4,2},{6,4},{8,6},{10,8},{12,10},{14,12},{16,14},{18,16},{20... | collective-permute-start | bytes 786440 | tf_op jit(solution)/shard_map/ppermute | solution.py:19
  68.7 13.5 %collective-permute-start.4 = (bf16[1,1024,128]{2,1,0:T(8,128)(2,1)S(1)}, bf16[1,1024,128]{2,1,0:T(8,128)(2,1)}, u32[]{:S(2)}, u32[]{:S(2)}) collective-permute-start(bf16[1,1024,128]{2,1,0:T(8,128)(2,1)S(1)} %bitcast.269), channel_id=1, source_target_pairs={{0,2},{2,4},{4,6},{6,8},{8,10},{10,12},{12,14},{14,16},{16,18},{18... | collective-permute-start | bytes 786440 | tf_op jit(solution)/shard_map/ppermute | solution.py:17
  73.8 10.1 %collective-permute-start.5 = (bf16[1,1024,128]{2,1,0:T(8,128)(2,1)S(1)}, bf16[1,1024,128]{2,1,0:T(8,128)(2,1)}, u32[]{:S(2)}, u32[]{:S(2)}) collective-permute-start(bf16[1,1024,128]{2,1,0:T(8,128)(2,1)S(1)} %bitcast.270), channel_id=1, source_target_pairs={{2,0},{4,2},{6,4},{8,6},{10,8},{12,10},{14,12},{16,14},{18,16},{20... | collective-permute-start | bytes 786440 | tf_op jit(solution)/shard_map/ppermute | solution.py:19
  98.1 13.6 %collective-permute-start.6 = (bf16[1,1024,128]{2,1,0:T(8,128)(2,1)S(1)}, bf16[1,1024,128]{2,1,0:T(8,128)(2,1)S(1)}, u32[]{:S(2)}, u32[]{:S(2)}) collective-permute-start(bf16[1,1024,128]{2,1,0:T(8,128)(2,1)S(1)} %bitcast.275), channel_id=1, source_target_pairs={{0,2},{2,4},{4,6},{6,8},{8,10},{10,12},{12,14},{14,16},{16,18},{18... | collective-permute-start | bytes 786440 | tf_op jit(solution)/shard_map/ppermute | solution.py:17
  103.3 9.2 %collective-permute-start.7 = (bf16[1,1024,128]{2,1,0:T(8,128)(2,1)S(1)}, bf16[1,1024,128]{2,1,0:T(8,128)(2,1)S(1)}, u32[]{:S(2)}, u32[]{:S(2)}) collective-permute-start(bf16[1,1024,128]{2,1,0:T(8,128)(2,1)S(1)} %bitcast.276), channel_id=1, source_target_pairs={{2,0},{4,2},{6,4},{8,6},{10,8},{12,10},{14,12},{16,14},{18,16},{20... | collective-permute-start | bytes 786440 | tf_op jit(solution)/shard_map/ppermute | solution.py:19
  121.1 2.1 copy-start.3
  125.6 14.4 %collective-permute-start.8 = (bf16[1,1024,128]{2,1,0:T(8,128)(2,1)S(1)}, bf16[1,1024,128]{2,1,0:T(8,128)(2,1)S(1)}, u32[]{:S(2)}, u32[]{:S(2)}) collective-permute-start(bf16[1,1024,128]{2,1,0:T(8,128)(2,1)S(1)} %bitcast.277), channel_id=1, source_target_pairs={{0,2},{2,4},{4,6},{6,8},{8,10},{10,12},{12,14},{14,16},{16,18},{18... | collective-permute-start | bytes 786440 | tf_op jit(solution)/shard_map/ppermute | solution.py:17
  131.6 9.2 %collective-permute-start.9 = (bf16[1,1024,128]{2,1,0:T(8,128)(2,1)S(1)}, bf16[1,1024,128]{2,1,0:T(8,128)(2,1)S(1)}, u32[]{:S(2)}, u32[]{:S(2)}) collective-permute-start(bf16[1,1024,128]{2,1,0:T(8,128)(2,1)S(1)} %bitcast.278), channel_id=1, source_target_pairs={{2,0},{4,2},{6,4},{8,6},{10,8},{12,10},{14,12},{16,14},{18,16},{20... | collective-permute-start | bytes 786440 | tf_op jit(solution)/shard_map/ppermute | solution.py:19
  151.9 58.7 %copy-start.2 = (f32[1024,128]{1,0:T(8,128)}, f32[1024,128]{1,0:T(8,128)S(1)}, u32[]{:S(2)}) copy-start(f32[1024,128]{1,0:T(8,128)S(1)} %get-tuple-element.27) | copy-start | bytes 1572868
  151.9 15.2 %collective-permute-start.10 = (bf16[1,1024,128]{2,1,0:T(8,128)(2,1)S(1)}, bf16[1,1024,128]{2,1,0:T(8,128)(2,1)}, u32[]{:S(2)}, u32[]{:S(2)}) collective-permute-start(bf16[1,1024,128]{2,1,0:T(8,128)(2,1)S(1)} %bitcast.279), channel_id=1, source_target_pairs={{0,2},{2,4},{4,6},{6,8},{8,10},{10,12},{12,14},{14,16},{16,18},{18... | collective-permute-start | bytes 786440 | tf_op jit(solution)/shard_map/ppermute | solution.py:17
  158.7 10.1 %collective-permute-start.11 = (bf16[1,1024,128]{2,1,0:T(8,128)(2,1)S(1)}, bf16[1,1024,128]{2,1,0:T(8,128)(2,1)}, u32[]{:S(2)}, u32[]{:S(2)}) collective-permute-start(bf16[1,1024,128]{2,1,0:T(8,128)(2,1)S(1)} %bitcast.280), channel_id=1, source_target_pairs={{2,0},{4,2},{6,4},{8,6},{10,8},{12,10},{14,12},{16,14},{18,16},{20... | collective-permute-start | bytes 786440 | tf_op jit(solution)/shard_map/ppermute | solution.py:19
  182.8 14.6 %collective-permute-start.12 = (bf16[1,1024,128]{2,1,0:T(8,128)(2,1)S(1)}, bf16[1,1024,128]{2,1,0:T(8,128)(2,1)}, u32[]{:S(2)}, u32[]{:S(2)}) collective-permute-start(bf16[1,1024,128]{2,1,0:T(8,128)(2,1)S(1)} %bitcast.281), channel_id=1, source_target_pairs={{0,2},{2,4},{4,6},{6,8},{8,10},{10,12},{12,14},{14,16},{16,18},{18... | collective-permute-start | bytes 786440 | tf_op jit(solution)/shard_map/ppermute | solution.py:17
  188.8 10.3 %collective-permute-start.13 = (bf16[1,1024,128]{2,1,0:T(8,128)(2,1)S(1)}, bf16[1,1024,128]{2,1,0:T(8,128)(2,1)}, u32[]{:S(2)}, u32[]{:S(2)}) collective-permute-start(bf16[1,1024,128]{2,1,0:T(8,128)(2,1)S(1)} %bitcast.282), channel_id=1, source_target_pairs={{2,0},{4,2},{6,4},{8,6},{10,8},{12,10},{14,12},{16,14},{18,16},{20... | collective-permute-start | bytes 786440 | tf_op jit(solution)/shard_map/ppermute | solution.py:19
  212.9 13.7 %collective-permute-start.14 = (bf16[1,1024,128]{2,1,0:T(8,128)(2,1)S(1)}, bf16[1,1024,128]{2,1,0:T(8,128)(2,1)S(1)}, u32[]{:S(2)}, u32[]{:S(2)}) collective-permute-start(bf16[1,1024,128]{2,1,0:T(8,128)(2,1)S(1)} %bitcast.267), channel_id=1, source_target_pairs={{0,2},{2,4},{4,6},{6,8},{8,10},{10,12},{12,14},{14,16},{16,18},{18... | collective-permute-start | bytes 786440 | tf_op jit(solution)/shard_map/ppermute | solution.py:17
  218.2 9.2 %collective-permute-start.15 = (bf16[1,1024,128]{2,1,0:T(8,128)(2,1)S(1)}, bf16[1,1024,128]{2,1,0:T(8,128)(2,1)S(1)}, u32[]{:S(2)}, u32[]{:S(2)}) collective-permute-start(bf16[1,1024,128]{2,1,0:T(8,128)(2,1)S(1)} %bitcast.268), channel_id=1, source_target_pairs={{2,0},{4,2},{6,4},{8,6},{10,8},{12,10},{14,12},{16,14},{18,16},{20... | collective-permute-start | bytes 786440 | tf_op jit(solution)/shard_map/ppermute | solution.py:19
  238.0 15.3 %collective-permute-start.16 = (bf16[1,1024,128]{2,1,0:T(8,128)(2,1)S(1)}, bf16[1,1024,128]{2,1,0:T(8,128)(2,1)S(1)}, u32[]{:S(2)}, u32[]{:S(2)}) collective-permute-start(bf16[1,1024,128]{2,1,0:T(8,128)(2,1)S(1)} %bitcast.265), channel_id=1, source_target_pairs={{0,2},{2,4},{4,6},{6,8},{8,10},{10,12},{12,14},{14,16},{16,18},{18... | collective-permute-start | bytes 786440 | tf_op jit(solution)/shard_map/ppermute | solution.py:17
  243.2 10.2 %collective-permute-start.17 = (bf16[1,1024,128]{2,1,0:T(8,128)(2,1)S(1)}, bf16[1,1024,128]{2,1,0:T(8,128)(2,1)S(1)}, u32[]{:S(2)}, u32[]{:S(2)}) collective-permute-start(bf16[1,1024,128]{2,1,0:T(8,128)(2,1)S(1)} %bitcast.266), channel_id=1, source_target_pairs={{2,0},{4,2},{6,4},{8,6},{10,8},{12,10},{14,12},{16,14},{18,16},{20... | collective-permute-start | bytes 786440 | tf_op jit(solution)/shard_map/ppermute | solution.py:19
  395.0 26.3 %copy-start.6 = (f32[128,128]{1,0:T(8,128)S(1)}, f32[128,128]{1,0:T(8,128)}, u32[]{:S(2)}) copy-start(f32[128,128]{1,0:T(8,128)} %get-tuple-element.3) | copy-start | bytes 196612
  (2 other events, 3.2 us)
Sparse Core Ops, SparseCore 0:
  266.0 128.9 all-reduce.2
where the time goes:
time: 432 us; the launch traced here: 429 us
  waiting for transfers between devices  129 us (30%)
  local copies, waits for them, and re-layouts  67.9 us (16%)
  blocking collectives  64.9 us (15%)
  other arithmetic  59.2 us (14%)
  starting transfers between devices  57.9 us (13%)
  matrix products  32.6 us (8%)
  between operations  17.6 us (4%)
    psum x1, waiting for transfers between devices, per_device(): gram = lax.psum(gram_local, ('row', 'col'))  129 us
    all_gather x9, blocking collectives, coupled(): line = lax.all_gather(rounded[None], 'col', axis=0, tiled=True)  64.9 us
    ppermute x9, starting transfers between devices, with_halo(): lax.ppermute(tail, axis, [(i, (i + 1) % count) for i in range(ends)])  46.3 us
    gather x9, local copies, waits for them, and re-layouts, coupled(): picked = stack[tile_cols]  28.6 us
    unnamed x18, other arithmetic  26.7 us
    dot_general x9, matrix products, coupled(): jnp.einsum('psab,psbk->pak', couplings, picked, preferred_element_type=jn...  26.4 us
    unnamed x32, local copies, waits for them, and re-layouts  20.4 us
    dot_general x9, local copies, waits for them, and re-layouts, coupled(): jnp.einsum('psab,psbk->pak', couplings, picked, preferred_element_type=jn...  16.6 us
  transfers between devices with their start and end apart: 19, of which 1 were waited for; matrix products, arithmetic and copies ran while one was open for 3% of the time, Pallas kernels for 0%

commit v1 on v0

v1 whole, which is shorter than its diff:
```python
import functools

import jax
import jax.numpy as jnp
from jax import lax
from jax.experimental import pallas as pl
from jax.experimental.pallas import tpu as pltpu
from jax.sharding import PartitionSpec as P

DEGREE = 8
SUB = 8
CHAINS = 2
VMEM = pl.BlockSpec(memory_space=pltpu.VMEM)
SMEM = pl.BlockSpec(memory_space=pltpu.SMEM)
ANY = pl.BlockSpec(memory_space=pl.ANY)
PARAMS = pltpu.CompilerParams(vmem_limit_bytes=16 << 20)
f32, bf16 = jnp.float32, jnp.bfloat16
shape_of = jax.ShapeDtypeStruct


def matmul_high(left, right, dims):
    return lax.dot_general(
        left,
        right,
        (dims, ((), ())),
        precision=lax.Precision.HIGHEST,
        preferred_element_type=f32,
    )


def pairing(count, first):
    pairs = []
    for i in range(first, count - 1, 2):
        pairs += [(i, i + 1), (i + 1, i)]
    if pairs and first:
        pairs += [(0, count - 1), (count - 1, 0)]
    return pairs


PAIRINGS = (("col", 0), ("row", 1), ("row", 0), ("col", 1))


def used_pairings():
    return [(a, f) for a, f in PAIRINGS if pairing(lax.axis_size(a), f)]


def exchange(rounded):
    received = [
        lax.ppermute(rounded, axis, pairing(lax.axis_size(axis), first))
        for axis, first in used_pairings()
    ]
    return [rounded] + received


def slot_table():
    places = {key: i + 1 for i, key in enumerate(used_pairings())}
    nowhere = len(places) + 1
    slots = [0]
    for axis in ("row", "col"):
        here, count = lax.axis_index(axis), lax.axis_size(axis)
        even, odd = places.get((axis, 0), nowhere), places.get((axis, 1), nowhere)
        is_even = here % 2 == 0
        slots += [
            jnp.where(here > 0, jnp.where(is_even, odd, even), nowhere),
            jnp.where(here < count - 1, jnp.where(is_even, even, odd), nowhere),
        ]
    return [jnp.asarray(s, jnp.int32) for s in slots], nowhere


def fill(stack, blocks, per_block):
    tile_size = stack.shape[2]
    for i, block in enumerate(blocks):
        for t in range(per_block):
            stack[i * per_block + t] = block[:, t * tile_size : (t + 1) * tile_size]
    stack[len(blocks) * per_block] = jnp.zeros(stack.shape[1:], stack.dtype)


def coupled(table, couplings, stack, p):
    total = None
    for s in range(couplings.shape[1]):
        part = lax.dot_general(
            stack[table[p, s]],
            couplings[p, s],
            (((1,), (1,)), ((), ())),
            preferred_element_type=f32,
        )
        total = part if total is None else total + part
    return total


def prepare_kernel(start, *outs):
    flipped = start[...].T
    rows = outs[0].shape[0]
    for c in range(len(outs) // 2):
        piece = flipped[c * rows : (c + 1) * rows, :]
        outs[2 * c][...] = piece
        outs[2 * c + 1][...] = piece.astype(bf16)


def load_kernel(source, target, sem):
    copy = pltpu.make_async_copy(source, target, sem)
    copy.start()
    copy.wait()


def step_kernel(halo, order, first, table, coef, couplings, *refs):
    blocks, refs = refs[:halo], refs[halo:]
    if first:
        now, a, b, out, rounded, stack = refs
        before = None
    else:
        now, before, a, b, out, rounded, stack = refs
    per_block, _, tile_size, _ = couplings.shape
    fill(stack, blocks, per_block)
    scale, center, keep = coef[0, order], coef[1, order], coef[2, order]
    for p in range(per_block):
        here = pl.ds(p * tile_size, tile_size)
        product = coupled(table, couplings, stack, p)
        vectors = now[:, here]
        following = scale * ((a[:, here] * vectors - product) * b[:, here] - center * vectors)
        if before is not None:
            following = following - keep * before[:, here]
        out[:, here] = following
        rounded[:, here] = following.astype(bf16)


def gram_kernel(chains, weights, *refs):
    parts, (out, full) = refs[:chains], refs[chains:]
    rows = parts[0].shape[0]
    for c in range(chains):
        full[pl.ds(c * rows, rows), :] = parts[c][...]
    vectors = full[...]
    out[...] = matmul_high(vectors, weights[...] * vectors, ((1,), (1,)))


def project_kernel(halo, chains, chain, nodes, table, couplings, *refs):
    blocks, parts = refs[:halo], refs[halo : halo + chains]
    a, out, stack, full, stiffed = refs[halo + chains :]
    per_block, _, tile_size, _ = couplings.shape
    fill(stack, blocks, per_block)
    rows = parts[0].shape[0]
    for c in range(chains):
        full[pl.ds(c * rows, rows), :] = parts[c][...]
    for p in range(per_block):
        here = pl.ds(p * tile_size, tile_size)
        product = coupled(table, couplings, stack, p)
        stiffed[:, here] = (a[:, here] * parts[chain][:, here] - product) / nodes
    out[...] = matmul_high(stiffed[...], full[...], ((1,), (1,)))


def final_kernel(chains, parity, mine, other, *refs):
    parts, (basis, ritz, full, work, inverse) = refs[:chains], refs[chains:]
    width = mine.shape[0]
    vec_rows = parts[0].shape[0]
    for c in range(chains):
        full[pl.ds(c * vec_rows, vec_rows), :] = parts[c][...]
    is_even = parity[0] == 0
    first, second = mine[...], other[...]
    rows = lax.broadcasted_iota(jnp.int32, (width, width), 0)
    lanes = lax.broadcasted_iota(jnp.int32, (width, width), 1)
    work[0] = jnp.where(is_even, first, second)
    work[1] = jnp.where(rows == lanes, 1.0, 0.0)
    sub = lax.broadcasted_iota(jnp.int32, (SUB, width), 0)

    def spread(value, i):
        return jnp.broadcast_to(value[i : i + 1, :], (SUB, width))

    def column(value, i):
        return jnp.broadcast_to(value[:, i : i + 1], (SUB, width))

    for k in range(width // SUB):
        here = pl.ds(k * SUB, SUB)
        left, right = work[0, here, :], work[1, here, :]
        cols = [column(left, k * SUB + i) for i in range(SUB)]
        lefts, rights, factors = [], [], []
        for i in range(SUB):
            pivot = spread(cols[i], i)
            root = lax.rsqrt(pivot)
            root = root * (1.5 - 0.5 * pivot * root * root)
            row_left, row_right = spread(left, i) * root, spread(right, i) * root
            row_cols = [spread(cols[m], i) * root if m > i else None for m in range(SUB)]
            lefts.append(row_left)
            rights.append(row_right)
            factors.append((root, row_cols))
            if i + 1 < SUB:
                scaled = jnp.where(sub > i, cols[i] * root, 0.0)
                left = left - scaled * row_left
                right = right - scaled * row_right
                for m in range(i + 1, SUB):
                    cols[m] = cols[m] - scaled * row_cols[m]
        done = rights[0]
        for i in range(1, SUB):
            done = jnp.where(sub == i, rights[i], done)
        inverse[here, :] = done
        for below in range(k + 1, width // SUB):
            there = pl.ds(below * SUB, SUB)
            left, right = work[0, there, :], work[1, there, :]
            cols = [column(left, k * SUB + i) for i in range(SUB)]
            for i in range(SUB):
                root, row_cols = factors[i]
                scaled = cols[i] * root
                left = left - scaled * lefts[i]
                right = right - scaled * rights[i]
                for m in range(i + 1, SUB):
                    cols[m] = cols[m] - scaled * row_cols[m]
            work[0, there, :] = left
            work[1, there, :] = right
    lower = inverse[...]
    basis[...] = matmul_high(full[...], lower, ((0,), (1,)))
    projected = jnp.where(is_even, second, first)
    half = matmul_high(lower, projected, ((1,), (1,)))
    ritz[...] = matmul_high(half, lower, ((1,), (1,)))


def call(kernel, outs, specs, args, scratch=(), flops=0, size=1 << 20, name=None):
    return pl.pallas_call(
        kernel,
        out_shape=outs,
        in_specs=specs + [VMEM] * (len(args) - len(specs)),
        out_specs=jax.tree.map(lambda _: VMEM, outs),
        scratch_shapes=list(scratch),
        compiler_params=PARAMS,
        cost_estimate=pl.CostEstimate(flops=flops, bytes_accessed=size, transcendentals=0),
        name=name,
    )(*args)


def per_device(start, couplings, tile_cols, stiffness, masses, bounds):
    rows_dev, width = start.shape
    per_block, stored, tile_size, _ = couplings.shape
    node_count = rows_dev * lax.axis_size("row") * lax.axis_size("col")
    rows = width // CHAINS
    wide, narrow = shape_of((rows, rows_dev), f32), shape_of((rows, rows_dev), bf16)
    flops = 2 * per_block * stored * tile_size * tile_size * rows

    prepared = call(prepare_kernel, (wide, narrow) * CHAINS, [], [start], flops=1 << 20, name="prepare")
    now, rounded = list(prepared[0::2]), list(prepared[1::2])
    before = [None] * CHAINS
    couplings = call(
        load_kernel,
        shape_of(couplings.shape, couplings.dtype),
        [ANY],
        [couplings],
        [pltpu.SemaphoreType.DMA],
        flops=1 << 28,
        name="load",
    )

    slots, nowhere = slot_table()
    block_of, tile_of = tile_cols // per_block, tile_cols % per_block
    slot = jnp.zeros_like(block_of)
    for q in range(1, 5):
        slot = jnp.where(block_of == q, slots[q], slot)
    table = slot * per_block + jnp.where(slot == nowhere, 0, tile_of)

    a, inverse_mass = stiffness[None, :], (1.0 / masses)[None, :]
    weights = (masses / node_count)[None, :]

    cut_low, cut_high = bounds[0], bounds[1]
    center = 0.5 * (cut_high + cut_low)
    radius = 0.5 * (cut_high - cut_low)
    scale = -radius / center
    twice_inverse = 2.0 / scale
    coefs = [(scale / radius, center, jnp.zeros((), f32))]
    for _ in range(DEGREE - 1):
        following = 1.0 / (twice_inverse - scale)
        coefs.append((2.0 * following / radius, center, scale * following))
        scale = following
    coef = jnp.stack([jnp.stack(list(c)) for c in zip(*coefs)])

    stack = pltpu.VMEM((nowhere * per_block + 1, rows, tile_size), bf16)

    for order in range(DEGREE):
        for c in range(CHAINS):
            blocks = exchange(rounded[c])
            old = [] if before[c] is None else [before[c]]
            args = [table, coef, couplings, *blocks, now[c], *old, a, inverse_mass]
            following, rounded[c] = call(
                functools.partial(step_kernel, len(blocks), order, not old),
                (wide, narrow),
                [SMEM, SMEM],
                args,
                [stack],
                flops=flops,
                name=f"step{order}",
            )
            before[c], now[c] = now[c], following

    full = pltpu.VMEM((width, rows_dev), f32)
    gram = call(
        functools.partial(gram_kernel, CHAINS),
        shape_of((width, width), f32),
        [],
        [weights, *now],
        [full],
        flops=flops,
        name="gram",
    )
    parts = []
    for c in range(CHAINS):
        blocks = exchange(rounded[c])
        parts.append(
            call(
                functools.partial(project_kernel, len(blocks), CHAINS, c, node_count),
                shape_of((rows, width), f32),
                [SMEM],
                [table, couplings, *blocks, *now, a],
                [stack, full, pltpu.VMEM((rows, rows_dev), f32)],
                flops=flops,
                name="project",
            )
        )
    projected = jnp.concatenate(parts, axis=0)

    parity = lax.axis_index("row") % 2
    swap = pairing(lax.axis_size("row"), 0)
    keep = jnp.where(parity == 0, gram, projected)
    send = jnp.where(parity == 0, projected, gram)
    mine = keep + lax.ppermute(send, "row", swap)
    for axis, bit in (("row", 2), ("col", 1)):
        count = lax.axis_size(axis)
        while bit < count:
            mine = mine + lax.ppermute(mine, axis, [(i, i ^ bit) for i in range(count)])
            bit *= 2
    other = lax.ppermute(mine, "row", swap)

    return call(
        functools.partial(final_kernel, CHAINS),
        (shape_of((rows_dev, width), f32), shape_of((width, width), f32)),
        [SMEM],
        [parity[None], mine, other, *now],
        [full, pltpu.VMEM((2, width, width), f32), pltpu.VMEM((width, width), f32)],
        flops=flops,
        name="final",
    )


def solution(mesh):
    for axis in ("row", "col"):
        count = mesh.shape[axis]
        if count & (count - 1) or count < 2:
            raise ValueError("axis size")
    return jax.shard_map(
        per_device,
        mesh=mesh,
        in_specs=(
            P(("row", "col"), None),
            P(("row", "col"), None, None, None),
            P(("row", "col"), None),
            P(("row", "col")),
            P(("row", "col")),
            P(),
        ),
        out_specs=(P(("row", "col"), None), P()),
        check_vma=False,
    )
```

time: 432 us -> 134 us (0.31)
  waiting for transfers between devices: 129 us -> 27.7 us
  blocking collectives: 64.9 us -> 0 us
  local copies, waits for them, and re-layouts: 67.9 us -> 4.35 us
  other arithmetic: 59.2 us -> 1.54 us
  Pallas kernels: 0 us -> 37 us
  matrix products: 32.6 us -> 0 us
  between operations: 17.6 us -> 4.33 us
    psum x1 -> x0, waiting for transfers between devices: 129 us -> none  [per_device(): gram = lax.psum(gram_local, ('row', 'col'))]
    all_gather x9 -> x0, blocking collectives: 64.9 us -> none  [coupled(): line = lax.all_gather(rounded[None], 'col', axis=0, tiled=True)]
    pallas_call x0 -> x22, Pallas kernels: none -> 37 us  [call(): pl.pallas_call(kernel, out_shape=outs, in_specs=specs + [VMEM] * (len(arg...]
    dot_general x14 -> x0, matrix products: 32.3 us -> none  [the longest x9 26.4 us: coupled(): jnp.einsum('psab,psbk->pak', couplings, picked, preferred_element_type=jn...]
    another operation x14 -> x1, other arithmetic: 29 us -> 0.07 us  [per_device(): coef = jnp.stack([jnp.stack(list(c)) for c in zip(*coefs)])]
    gather x9 -> x0, local copies, waits for them, and re-layouts: 28.6 us -> none  [coupled(): picked = stack[tile_cols]]
    ppermute x18 -> x60, waiting for transfers between devices: 0.05 us -> 27.7 us  [the longest x4 17.4 us: per_device(): mine = mine + lax.ppermute(mine, axis, [(i, i ^ bit) for i in range(count)])]
    unnamed x18 -> x0, other arithmetic: 26.7 us -> none
  transfers between devices with their start and end apart: 19 -> 60, of which waited for: 1 -> 14; matrix products, arithmetic and copies ran while one was open for 3% -> 2% of each run, Pallas kernels for 0% -> 21%
where the time goes in v1:
time: 134 us
  starting transfers between devices  59.1 us (44%)
  Pallas kernels  37 us (28%)
  waiting for transfers between devices  27.7 us (21%)
  local copies, waits for them, and re-layouts  4.35 us (3%)
  between operations  4.33 us (3%)
  other arithmetic  1.54 us (1%)
    ppermute x54, starting transfers between devices, exchange(): lax.ppermute(rounded, axis, pairing(lax.axis_size(axis), first))  58 us
    pallas_call x22, Pallas kernels, call(): pl.pallas_call(kernel, out_shape=outs, in_specs=specs + [VMEM] * (len(arg...  37 us
    ppermute x4, waiting for transfers between devices, per_device(): mine = mine + lax.ppermute(mine, axis, [(i, i ^ bit) for i in range(count)])  17.4 us
    ppermute x54, waiting for transfers between devices, exchange(): lax.ppermute(rounded, axis, pairing(lax.axis_size(axis), first))  7.79 us
    unnamed x6, local copies, waits for them, and re-layouts  2.78 us
  transfers between devices with their start and end apart: 60, of which 14 were waited for; matrix products, arithmetic and copies ran while one was open for 2% of the time, Pallas kernels for 21%

profile of v1, /device:TPU:0, one launch (start us, length us, event | category | flops | bytes accessed | tf_op | source)
XLA Modules:
  0.0 134.0 jit_solution(18276447554817190046)
XLA Ops:
  1.9 3.0 %collective-permute-start = (bf16[64,1024]{1,0:T(8,128)(2,1)S(1)}, bf16[64,1024]{1,0:T(8,128)(2,1)S(1)}, u32[]{:S(2)}, u32[]{:S(2)}) collective-permute-start(bf16[64,1024]{1,0:T(8,128)(2,1)S(1)} %get-tuple-element.38.refs_0_), channel_id=1, source_target_pairs={{0,1},{1,0},{2,3},{3,2},{4,5},{5,4},{6,7},{7,6},{8,9},{9,8},{10,11... | collective-permute-start | bytes 393224 | tf_op jit(solution)/shard_map/ppermute | solution.py:49
  4.9 3.7 %collective-permute-start.1 = (bf16[64,1024]{1,0:T(8,128)(2,1)S(1)}, bf16[64,1024]{1,0:T(8,128)(2,1)S(1)}, u32[]{:S(2)}, u32[]{:S(2)}) collective-permute-start(bf16[64,1024]{1,0:T(8,128)(2,1)S(1)} %get-tuple-element.38.refs_0_), channel_id=1, source_target_pairs={{2,4},{4,2},{6,8},{8,6},{10,12},{12,10},{14,16},{16,14},{18,20},{2... | collective-permute-start | bytes 393224 | tf_op jit(solution)/shard_map/ppermute | solution.py:49
  15.7 1.7 %copy-done = bf16[4,5,256,256]{3,2,1,0:T(8,128)(2,1)S(1)} copy-done((bf16[4,5,256,256]{3,2,1,0:T(8,128)(2,1)S(1)}, bf16[4,5,256,256]{3,2,1,0:T(8,128)(2,1)}, u32[]{:S(2)}) %copy-start) | copy-done | bytes 2621464
  19.8 1.8 %collective-permute-start.27 = (bf16[64,1024]{1,0:T(8,128)(2,1)S(1)}, bf16[64,1024]{1,0:T(8,128)(2,1)S(1)}, u32[]{:S(2)}, u32[]{:S(2)}) collective-permute-start(bf16[64,1024]{1,0:T(8,128)(2,1)S(1)} %get-tuple-element.57.refs_0_), channel_id=1, source_target_pairs={{0,1},{1,0},{2,3},{3,2},{4,5},{5,4},{6,7},{7,6},{8,9},{9,8},{10,11... | collective-permute-start | bytes 393224 | tf_op jit(solution)/shard_map/ppermute | solution.py:49
  21.6 3.7 %collective-permute-start.28 = (bf16[64,1024]{1,0:T(8,128)(2,1)S(1)}, bf16[64,1024]{1,0:T(8,128)(2,1)S(1)}, u32[]{:S(2)}, u32[]{:S(2)}) collective-permute-start(bf16[64,1024]{1,0:T(8,128)(2,1)S(1)} %get-tuple-element.57.refs_0_), channel_id=1, source_target_pairs={{2,4},{4,2},{6,8},{8,6},{10,12},{12,10},{14,16},{16,14},{18,20},{2... | collective-permute-start | bytes 393224 | tf_op jit(solution)/shard_map/ppermute | solution.py:49
  31.0 3.7 %collective-permute-start.31 = (bf16[64,1024]{1,0:T(8,128)(2,1)S(1)}, bf16[64,1024]{1,0:T(8,128)(2,1)S(1)}, u32[]{:S(2)}, u32[]{:S(2)}) collective-permute-start(bf16[64,1024]{1,0:T(8,128)(2,1)S(1)} %get-tuple-element.59.refs_0_), channel_id=1, source_target_pairs={{2,4},{4,2},{6,8},{8,6},{10,12},{12,10},{14,16},{16,14},{18,20},{2... | collective-permute-start | bytes 393224 | tf_op jit(solution)/shard_map/ppermute | solution.py:49
  34.8 1.5 %step1.2 = (f32[64,1024]{1,0:T(8,128)S(1)}, bf16[64,1024]{1,0:T(8,128)(2,1)S(1)}) custom-call(s32[4,5]{1,0:T(4,128)S(1)} %fusion.2.table, f32[3,8]{1,0:T(4,128)S(1)} %pad_maximum_fusion.1.coef, bf16[4,5,256,256]{3,2,1,0:T(8,128)(2,1)S(1)} %load.1.couplings, bf16[64,1024]{1,0:T(8,128)(2,1)S(1)} %get-tuple-element.40.refs_0_, ...), custom_call_target="tpu_custom_call" | custom-call | flops 167772160 | bytes 1048576 | tf_op jit(solution)/shard_map/step1/pallas_call | solution.py:216
  38.1 1.5 %step2.3 = (f32[64,1024]{1,0:T(8,128)S(1)}, bf16[64,1024]{1,0:T(8,128)(2,1)S(1)}) custom-call(s32[4,5]{1,0:T(4,128)S(1)} %fusion.2.table, f32[3,8]{1,0:T(4,128)S(1)} %pad_maximum_fusion.1.coef, bf16[4,5,256,256]{3,2,1,0:T(8,128)(2,1)S(1)} %load.1.couplings, bf16[64,1024]{1,0:T(8,128)(2,1)S(1)} %get-tuple-element.59.refs_0_, ...), custom_call_target="tpu_custom_call" | custom-call | flops 167772160 | bytes 1048576 | tf_op jit(solution)/shard_map/step2/pallas_call | solution.py:216
  41.0 3.4 %collective-permute-start.34 = (bf16[64,1024]{1,0:T(8,128)(2,1)S(1)}, bf16[64,1024]{1,0:T(8,128)(2,1)S(1)}, u32[]{:S(2)}, u32[]{:S(2)}) collective-permute-start(bf16[64,1024]{1,0:T(8,128)(2,1)S(1)} %get-tuple-element.61.refs_0_), channel_id=1, source_target_pairs={{2,4},{4,2},{6,8},{8,6},{10,12},{12,10},{14,16},{16,14},{18,20},{2... | collective-permute-start | bytes 393224 | tf_op jit(solution)/shard_map/ppermute | solution.py:49
  50.4 3.9 %collective-permute-start.37 = (bf16[64,1024]{1,0:T(8,128)(2,1)S(1)}, bf16[64,1024]{1,0:T(8,128)(2,1)S(1)}, u32[]{:S(2)}, u32[]{:S(2)}) collective-permute-start(bf16[64,1024]{1,0:T(8,128)(2,1)S(1)} %get-tuple-element.63.refs_0_), channel_id=1, source_target_pairs={{2,4},{4,2},{6,8},{8,6},{10,12},{12,10},{14,16},{16,14},{18,20},{2... | collective-permute-start | bytes 393224 | tf_op jit(solution)/shard_map/ppermute | solution.py:49
  54.4 1.5 %step3.2 = (f32[64,1024]{1,0:T(8,128)S(1)}, bf16[64,1024]{1,0:T(8,128)(2,1)S(1)}) custom-call(s32[4,5]{1,0:T(4,128)S(1)} %fusion.2.table, f32[3,8]{1,0:T(4,128)S(1)} %pad_maximum_fusion.1.coef, bf16[4,5,256,256]{3,2,1,0:T(8,128)(2,1)S(1)} %load.1.couplings, bf16[64,1024]{1,0:T(8,128)(2,1)S(1)} %get-tuple-element.44.refs_0_, ...), custom_call_target="tpu_custom_call" | custom-call | flops 167772160 | bytes 1048576 | tf_op jit(solution)/shard_map/step3/pallas_call | solution.py:216
  60.4 3.4 %collective-permute-start.40 = (bf16[64,1024]{1,0:T(8,128)(2,1)S(1)}, bf16[64,1024]{1,0:T(8,128)(2,1)S(1)}, u32[]{:S(2)}, u32[]{:S(2)}) collective-permute-start(bf16[64,1024]{1,0:T(8,128)(2,1)S(1)} %get-tuple-element.65.refs_0_), channel_id=1, source_target_pairs={{2,4},{4,2},{6,8},{8,6},{10,12},{12,10},{14,16},{16,14},{18,20},{2... | collective-permute-start | bytes 393224 | tf_op jit(solution)/shard_map/ppermute | solution.py:49
  69.8 4.1 %collective-permute-start.43 = (bf16[64,1024]{1,0:T(8,128)(2,1)S(1)}, bf16[64,1024]{1,0:T(8,128)(2,1)S(1)}, u32[]{:S(2)}, u32[]{:S(2)}) collective-permute-start(bf16[64,1024]{1,0:T(8,128)(2,1)S(1)} %get-tuple-element.67.refs_0_), channel_id=1, source_target_pairs={{2,4},{4,2},{6,8},{8,6},{10,12},{12,10},{14,16},{16,14},{18,20},{2... | collective-permute-start | bytes 393224 | tf_op jit(solution)/shard_map/ppermute | solution.py:49
  79.8 3.6 %collective-permute-start.46 = (bf16[64,1024]{1,0:T(8,128)(2,1)S(1)}, bf16[64,1024]{1,0:T(8,128)(2,1)S(1)}, u32[]{:S(2)}, u32[]{:S(2)}) collective-permute-start(bf16[64,1024]{1,0:T(8,128)(2,1)S(1)} %get-tuple-element.69.refs_0_), channel_id=1, source_target_pairs={{2,4},{4,2},{6,8},{8,6},{10,12},{12,10},{14,16},{16,14},{18,20},{2... | collective-permute-start | bytes 393224 | tf_op jit(solution)/shard_map/ppermute | solution.py:49
  89.4 4.1 %collective-permute-start.52 = (bf16[64,1024]{1,0:T(8,128)(2,1)S(1)}, bf16[64,1024]{1,0:T(8,128)(2,1)S(1)}, u32[]{:S(2)}, u32[]{:S(2)}) collective-permute-start(bf16[64,1024]{1,0:T(8,128)(2,1)S(1)} %get-tuple-element.73.refs_0_), channel_id=1, source_target_pairs={{2,4},{4,2},{6,8},{8,6},{10,12},{12,10},{14,16},{16,14},{18,20},{2... | collective-permute-start | bytes 393224 | tf_op jit(solution)/shard_map/ppermute | solution.py:49
  93.6 1.5 %step7.2 = (f32[64,1024]{1,0:T(8,128)S(1)}, bf16[64,1024]{1,0:T(8,128)(2,1)S(1)}) custom-call(s32[4,5]{1,0:T(4,128)S(1)} %fusion.2.table, f32[3,8]{1,0:T(4,128)S(1)} %pad_maximum_fusion.1.coef, bf16[4,5,256,256]{3,2,1,0:T(8,128)(2,1)S(1)} %load.1.couplings, bf16[64,1024]{1,0:T(8,128)(2,1)S(1)} %get-tuple-element.52.refs_0_, ...), custom_call_target="tpu_custom_call" | custom-call | flops 167772160 | bytes 1048576 | tf_op jit(solution)/shard_map/step7/pallas_call | solution.py:216
  97.4 2.1 %project.3 = f32[64,128]{1,0:T(8,128)S(1)} custom-call(s32[4,5]{1,0:T(4,128)S(1)} %fusion.2.table, bf16[4,5,256,256]{3,2,1,0:T(8,128)(2,1)S(1)} %load.1.couplings, bf16[64,1024]{1,0:T(8,128)(2,1)S(1)} %get-tuple-element.73.refs_0_, bf16[64,1024]{1,0:T(8,128)(2,1)S(1)} %collective-permute-done.51.refs_1_, ...), custom_call_target="tpu_custom_call" | custom-call | flops 167772160 | bytes 1048576 | tf_op jit(solution)/shard_map/project/pallas_call | solution.py:216
  101.1 2.6 %collective-permute-done.49.refs_2_ = bf16[64,1024]{1,0:T(8,128)(2,1)S(1)} collective-permute-done((bf16[64,1024]{1,0:T(8,128)(2,1)S(1)}, bf16[64,1024]{1,0:T(8,128)(2,1)S(1)}, u32[]{:S(2)}, u32[]{:S(2)}) %collective-permute-start.49) | collective-permute-done | bytes 131104 | tf_op jit(solution)/shard_map/ppermute | solution.py:49
  103.6 2.1 %project.2 = f32[64,128]{1,0:T(8,128)S(1)} custom-call(s32[4,5]{1,0:T(4,128)S(1)} %fusion.2.table, bf16[4,5,256,256]{3,2,1,0:T(8,128)(2,1)S(1)} %load.1.couplings, bf16[64,1024]{1,0:T(8,128)(2,1)S(1)} %get-tuple-element.72.refs_0_, bf16[64,1024]{1,0:T(8,128)(2,1)S(1)} %collective-permute-done.48.refs_1_, ...), custom_call_target="tpu_custom_call" | custom-call | flops 167772160 | bytes 1048576 | tf_op jit(solution)/shard_map/project/pallas_call | solution.py:216
  107.2 4.3 %collective-permute-done.55 = f32[128,128]{1,0:T(8,128)S(1)} collective-permute-done((f32[128,128]{1,0:T(8,128)S(1)}, f32[128,128]{1,0:T(8,128)S(1)}, u32[]{:S(2)}, u32[]{:S(2)}) %collective-permute-start.55) | collective-permute-done | bytes 65568 | tf_op jit(solution)/shard_map/ppermute | solution.py:323
  111.6 4.3 %collective-permute-done.56 = f32[128,128]{1,0:T(8,128)S(1)} collective-permute-done((f32[128,128]{1,0:T(8,128)S(1)}, f32[128,128]{1,0:T(8,128)S(1)}, u32[]{:S(2)}, u32[]{:S(2)}) %collective-permute-start.56) | collective-permute-done | bytes 65568 | tf_op jit(solution)/shard_map/ppermute | solution.py:323
  115.9 5.3 %collective-permute-done.57 = f32[128,128]{1,0:T(8,128)S(1)} collective-permute-done((f32[128,128]{1,0:T(8,128)S(1)}, f32[128,128]{1,0:T(8,128)S(1)}, u32[]{:S(2)}, u32[]{:S(2)}) %collective-permute-start.57) | collective-permute-done | bytes 65568 | tf_op jit(solution)/shard_map/ppermute | solution.py:323
  121.9 3.6 %collective-permute-done.58 = f32[128,128]{1,0:T(8,128)S(1)} collective-permute-done((f32[128,128]{1,0:T(8,128)S(1)}, f32[128,128]{1,0:T(8,128)S(1)}, u32[]{:S(2)}, u32[]{:S(2)}) %collective-permute-start.58) | collective-permute-done | bytes 65568 | tf_op jit(solution)/shard_map/ppermute | solution.py:323
  126.9 7.1 %final.1 = (f32[1024,128]{1,0:T(8,128)}, f32[128,128]{1,0:T(8,128)}) custom-call(s32[1]{0:T(128)} %bitcast.parity, f32[128,128]{1,0:T(8,128)S(1)} %add.49.mine, f32[128,128]{1,0:T(8,128)S(1)} %collective-permute-done.59.other, f32[64,1024]{1,0:T(8,128)S(1)} %get-tuple-element.54.refs_0_.refs_4_, f32[64,1024]{1,0:T(8,128)S(1)} %get-tuple-element.71.refs_1_.refs_5_), custom_call_target="tpu_custom_call" | custom-call | flops 167772160 | bytes 1048576 | tf_op jit(solution)/shard_map/final/pallas_call | solution.py:216
  (137 shorter events, 52.0 us)
Async XLA Ops:
  1.9 23.4 %collective-permute-start = (bf16[64,1024]{1,0:T(8,128)(2,1)S(1)}, bf16[64,1024]{1,0:T(8,128)(2,1)S(1)}, u32[]{:S(2)}, u32[]{:S(2)}) collective-permute-start(bf16[64,1024]{1,0:T(8,128)(2,1)S(1)} %get-tuple-element.38.refs_0_), channel_id=1, source_target_pairs={{0,1},{1,0},{2,3},{3,2},{4,5},{5,4},{6,7},{7,6},{8,9},{9,8},{10,11... | collective-permute-start | bytes 393224 | tf_op jit(solution)/shard_map/ppermute | solution.py:49
  4.9 20.4 %collective-permute-start.1 = (bf16[64,1024]{1,0:T(8,128)(2,1)S(1)}, bf16[64,1024]{1,0:T(8,128)(2,1)S(1)}, u32[]{:S(2)}, u32[]{:S(2)}) collective-permute-start(bf16[64,1024]{1,0:T(8,128)(2,1)S(1)} %get-tuple-element.38.refs_0_), channel_id=1, source_target_pairs={{2,4},{4,2},{6,8},{8,6},{10,12},{12,10},{14,16},{16,14},{18,20},{2... | collective-permute-start | bytes 393224 | tf_op jit(solution)/shard_map/ppermute | solution.py:49
  8.6 9.0 %collective-permute-start.24 = (bf16[64,1024]{1,0:T(8,128)(2,1)S(1)}, bf16[64,1024]{1,0:T(8,128)(2,1)S(1)}, u32[]{:S(2)}, u32[]{:S(2)}) collective-permute-start(bf16[64,1024]{1,0:T(8,128)(2,1)S(1)} %get-tuple-element.55.refs_0_), channel_id=1, source_target_pairs={{0,1},{1,0},{2,3},{3,2},{4,5},{5,4},{6,7},{7,6},{8,9},{9,8},{10,11... | collective-permute-start | bytes 393224 | tf_op jit(solution)/shard_map/ppermute | solution.py:49
  9.2 9.1 %collective-permute-start.25 = (bf16[64,1024]{1,0:T(8,128)(2,1)S(1)}, bf16[64,1024]{1,0:T(8,128)(2,1)S(1)}, u32[]{:S(2)}, u32[]{:S(2)}) collective-permute-start(bf16[64,1024]{1,0:T(8,128)(2,1)S(1)} %get-tuple-element.55.refs_0_), channel_id=1, source_target_pairs={{2,4},{4,2},{6,8},{8,6},{10,12},{12,10},{14,16},{16,14},{18,20},{2... | collective-permute-start | bytes 393224 | tf_op jit(solution)/shard_map/ppermute | solution.py:49
  9.4 8.9 %collective-permute-start.26 = (bf16[64,1024]{1,0:T(8,128)(2,1)S(1)}, bf16[64,1024]{1,0:T(8,128)(2,1)S(1)}, u32[]{:S(2)}, u32[]{:S(2)}) collective-permute-start(bf16[64,1024]{1,0:T(8,128)(2,1)S(1)} %get-tuple-element.55.refs_0_), channel_id=1, source_target_pairs={{0,2},{2,0},{4,6},{6,4},{8,10},{10,8},{12,14},{14,12},{16,18},{18,... | collective-permute-start | bytes 393224 | tf_op jit(solution)/shard_map/ppermute | solution.py:49
  17.7 7.7 %collective-permute-start.2 = (bf16[64,1024]{1,0:T(8,128)(2,1)S(1)}, bf16[64,1024]{1,0:T(8,128)(2,1)S(1)}, u32[]{:S(2)}, u32[]{:S(2)}) collective-permute-start(bf16[64,1024]{1,0:T(8,128)(2,1)S(1)} %get-tuple-element.38.refs_0_), channel_id=1, source_target_pairs={{0,2},{2,0},{4,6},{6,4},{8,10},{10,8},{12,14},{14,12},{16,18},{18,... | collective-permute-start | bytes 393224 | tf_op jit(solution)/shard_map/ppermute | solution.py:49
  19.8 8.1 %collective-permute-start.27 = (bf16[64,1024]{1,0:T(8,128)(2,1)S(1)}, bf16[64,1024]{1,0:T(8,128)(2,1)S(1)}, u32[]{:S(2)}, u32[]{:S(2)}) collective-permute-start(bf16[64,1024]{1,0:T(8,128)(2,1)S(1)} %get-tuple-element.57.refs_0_), channel_id=1, source_target_pairs={{0,1},{1,0},{2,3},{3,2},{4,5},{5,4},{6,7},{7,6},{8,9},{9,8},{10,11... | collective-permute-start | bytes 393224 | tf_op jit(solution)/shard_map/ppermute | solution.py:49
  26.9 7.9 %collective-permute-start.3 = (bf16[64,1024]{1,0:T(8,128)(2,1)S(1)}, bf16[64,1024]{1,0:T(8,128)(2,1)S(1)}, u32[]{:S(2)}, u32[]{:S(2)}) collective-permute-start(bf16[64,1024]{1,0:T(8,128)(2,1)S(1)} %get-tuple-element.40.refs_0_), channel_id=1, source_target_pairs={{0,1},{1,0},{2,3},{3,2},{4,5},{5,4},{6,7},{7,6},{8,9},{9,8},{10,11... | collective-permute-start | bytes 393224 | tf_op jit(solution)/shard_map/ppermute | solution.py:49
  27.5 7.3 %collective-permute-start.4 = (bf16[64,1024]{1,0:T(8,128)(2,1)S(1)}, bf16[64,1024]{1,0:T(8,128)(2,1)S(1)}, u32[]{:S(2)}, u32[]{:S(2)}) collective-permute-start(bf16[64,1024]{1,0:T(8,128)(2,1)S(1)} %get-tuple-element.40.refs_0_), channel_id=1, source_target_pairs={{2,4},{4,2},{6,8},{8,6},{10,12},{12,10},{14,16},{16,14},{18,20},{2... | collective-permute-start | bytes 393224 | tf_op jit(solution)/shard_map/ppermute | solution.py:49
  30.2 7.9 %collective-permute-start.30 = (bf16[64,1024]{1,0:T(8,128)(2,1)S(1)}, bf16[64,1024]{1,0:T(8,128)(2,1)S(1)}, u32[]{:S(2)}, u32[]{:S(2)}) collective-permute-start(bf16[64,1024]{1,0:T(8,128)(2,1)S(1)} %get-tuple-element.59.refs_0_), channel_id=1, source_target_pairs={{0,1},{1,0},{2,3},{3,2},{4,5},{5,4},{6,7},{7,6},{8,9},{9,8},{10,11... | collective-permute-start | bytes 393224 | tf_op jit(solution)/shard_map/ppermute | solution.py:49
  36.3 8.1 %collective-permute-start.6 = (bf16[64,1024]{1,0:T(8,128)(2,1)S(1)}, bf16[64,1024]{1,0:T(8,128)(2,1)S(1)}, u32[]{:S(2)}, u32[]{:S(2)}) collective-permute-start(bf16[64,1024]{1,0:T(8,128)(2,1)S(1)} %get-tuple-element.42.refs_0_), channel_id=1, source_target_pairs={{0,1},{1,0},{2,3},{3,2},{4,5},{5,4},{6,7},{7,6},{8,9},{9,8},{10,11... | collective-permute-start | bytes 393224 | tf_op jit(solution)/shard_map/ppermute | solution.py:49
  37.7 7.2 %collective-permute-start.7 = (bf16[64,1024]{1,0:T(8,128)(2,1)S(1)}, bf16[64,1024]{1,0:T(8,128)(2,1)S(1)}, u32[]{:S(2)}, u32[]{:S(2)}) collective-permute-start(bf16[64,1024]{1,0:T(8,128)(2,1)S(1)} %get-tuple-element.42.refs_0_), channel_id=1, source_target_pairs={{2,4},{4,2},{6,8},{8,6},{10,12},{12,10},{14,16},{16,14},{18,20},{2... | collective-permute-start | bytes 393224 | tf_op jit(solution)/shard_map/ppermute | solution.py:49
  39.6 8.0 %collective-permute-start.33 = (bf16[64,1024]{1,0:T(8,128)(2,1)S(1)}, bf16[64,1024]{1,0:T(8,128)(2,1)S(1)}, u32[]{:S(2)}, u32[]{:S(2)}) collective-permute-start(bf16[64,1024]{1,0:T(8,128)(2,1)S(1)} %get-tuple-element.61.refs_0_), channel_id=1, source_target_pairs={{0,1},{1,0},{2,3},{3,2},{4,5},{5,4},{6,7},{7,6},{8,9},{9,8},{10,11... | collective-permute-start | bytes 393224 | tf_op jit(solution)/shard_map/ppermute | solution.py:49
  46.5 7.9 %collective-permute-start.9 = (bf16[64,1024]{1,0:T(8,128)(2,1)S(1)}, bf16[64,1024]{1,0:T(8,128)(2,1)S(1)}, u32[]{:S(2)}, u32[]{:S(2)}) collective-permute-start(bf16[64,1024]{1,0:T(8,128)(2,1)S(1)} %get-tuple-element.44.refs_0_), channel_id=1, source_target_pairs={{0,1},{1,0},{2,3},{3,2},{4,5},{5,4},{6,7},{7,6},{8,9},{9,8},{10,11... | collective-permute-start | bytes 393224 | tf_op jit(solution)/shard_map/ppermute | solution.py:49
  49.6 7.9 %collective-permute-start.36 = (bf16[64,1024]{1,0:T(8,128)(2,1)S(1)}, bf16[64,1024]{1,0:T(8,128)(2,1)S(1)}, u32[]{:S(2)}, u32[]{:S(2)}) collective-permute-start(bf16[64,1024]{1,0:T(8,128)(2,1)S(1)} %get-tuple-element.63.refs_0_), channel_id=1, source_target_pairs={{0,1},{1,0},{2,3},{3,2},{4,5},{5,4},{6,7},{7,6},{8,9},{9,8},{10,11... | collective-permute-start | bytes 393224 | tf_op jit(solution)/shard_map/ppermute | solution.py:49
  55.9 7.9 %collective-permute-start.12 = (bf16[64,1024]{1,0:T(8,128)(2,1)S(1)}, bf16[64,1024]{1,0:T(8,128)(2,1)S(1)}, u32[]{:S(2)}, u32[]{:S(2)}) collective-permute-start(bf16[64,1024]{1,0:T(8,128)(2,1)S(1)} %get-tuple-element.46.refs_0_), channel_id=1, source_target_pairs={{0,1},{1,0},{2,3},{3,2},{4,5},{5,4},{6,7},{7,6},{8,9},{9,8},{10,11... | collective-permute-start | bytes 393224 | tf_op jit(solution)/shard_map/ppermute | solution.py:49
  59.1 8.2 %collective-permute-start.39 = (bf16[64,1024]{1,0:T(8,128)(2,1)S(1)}, bf16[64,1024]{1,0:T(8,128)(2,1)S(1)}, u32[]{:S(2)}, u32[]{:S(2)}) collective-permute-start(bf16[64,1024]{1,0:T(8,128)(2,1)S(1)} %get-tuple-element.65.refs_0_), channel_id=1, source_target_pairs={{0,1},{1,0},{2,3},{3,2},{4,5},{5,4},{6,7},{7,6},{8,9},{9,8},{10,11... | collective-permute-start | bytes 393224 | tf_op jit(solution)/shard_map/ppermute | solution.py:49
  66.1 7.9 %collective-permute-start.15 = (bf16[64,1024]{1,0:T(8,128)(2,1)S(1)}, bf16[64,1024]{1,0:T(8,128)(2,1)S(1)}, u32[]{:S(2)}, u32[]{:S(2)}) collective-permute-start(bf16[64,1024]{1,0:T(8,128)(2,1)S(1)} %get-tuple-element.48.refs_0_), channel_id=1, source_target_pairs={{0,1},{1,0},{2,3},{3,2},{4,5},{5,4},{6,7},{7,6},{8,9},{9,8},{10,11... | collective-permute-start | bytes 393224 | tf_op jit(solution)/shard_map/ppermute | solution.py:49
  69.0 7.9 %collective-permute-start.42 = (bf16[64,1024]{1,0:T(8,128)(2,1)S(1)}, bf16[64,1024]{1,0:T(8,128)(2,1)S(1)}, u32[]{:S(2)}, u32[]{:S(2)}) collective-permute-start(bf16[64,1024]{1,0:T(8,128)(2,1)S(1)} %get-tuple-element.67.refs_0_), channel_id=1, source_target_pairs={{0,1},{1,0},{2,3},{3,2},{4,5},{5,4},{6,7},{7,6},{8,9},{9,8},{10,11... | collective-permute-start | bytes 393224 | tf_op jit(solution)/shard_map/ppermute | solution.py:49
  75.5 7.9 %collective-permute-start.18 = (bf16[64,1024]{1,0:T(8,128)(2,1)S(1)}, bf16[64,1024]{1,0:T(8,128)(2,1)S(1)}, u32[]{:S(2)}, u32[]{:S(2)}) collective-permute-start(bf16[64,1024]{1,0:T(8,128)(2,1)S(1)} %get-tuple-element.50.refs_0_), channel_id=1, source_target_pairs={{0,1},{1,0},{2,3},{3,2},{4,5},{5,4},{6,7},{7,6},{8,9},{9,8},{10,11... | collective-permute-start | bytes 393224 | tf_op jit(solution)/shard_map/ppermute | solution.py:49
  78.5 8.3 %collective-permute-start.45 = (bf16[64,1024]{1,0:T(8,128)(2,1)S(1)}, bf16[64,1024]{1,0:T(8,128)(2,1)S(1)}, u32[]{:S(2)}, u32[]{:S(2)}) collective-permute-start(bf16[64,1024]{1,0:T(8,128)(2,1)S(1)} %get-tuple-element.69.refs_0_), channel_id=1, source_target_pairs={{0,1},{1,0},{2,3},{3,2},{4,5},{5,4},{6,7},{7,6},{8,9},{9,8},{10,11... | collective-permute-start | bytes 393224 | tf_op jit(solution)/shard_map/ppermute | solution.py:49
  85.7 7.9 %collective-permute-start.21 = (bf16[64,1024]{1,0:T(8,128)(2,1)S(1)}, bf16[64,1024]{1,0:T(8,128)(2,1)S(1)}, u32[]{:S(2)}, u32[]{:S(2)}) collective-permute-start(bf16[64,1024]{1,0:T(8,128)(2,1)S(1)} %get-tuple-element.52.refs_0_), channel_id=1, source_target_pairs={{0,1},{1,0},{2,3},{3,2},{4,5},{5,4},{6,7},{7,6},{8,9},{9,8},{10,11... | collective-permute-start | bytes 393224 | tf_op jit(solution)/shard_map/ppermute | solution.py:49
  88.4 8.1 %collective-permute-start.51 = (bf16[64,1024]{1,0:T(8,128)(2,1)S(1)}, bf16[64,1024]{1,0:T(8,128)(2,1)S(1)}, u32[]{:S(2)}, u32[]{:S(2)}) collective-permute-start(bf16[64,1024]{1,0:T(8,128)(2,1)S(1)} %get-tuple-element.73.refs_0_), channel_id=1, source_target_pairs={{0,1},{1,0},{2,3},{3,2},{4,5},{5,4},{6,7},{7,6},{8,9},{9,8},{10,11... | collective-permute-start | bytes 393224 | tf_op jit(solution)/shard_map/ppermute | solution.py:49
  89.4 8.0 %collective-permute-start.52 = (bf16[64,1024]{1,0:T(8,128)(2,1)S(1)}, bf16[64,1024]{1,0:T(8,128)(2,1)S(1)}, u32[]{:S(2)}, u32[]{:S(2)}) collective-permute-start(bf16[64,1024]{1,0:T(8,128)(2,1)S(1)} %get-tuple-element.73.refs_0_), channel_id=1, source_target_pairs={{2,4},{4,2},{6,8},{8,6},{10,12},{12,10},{14,16},{16,14},{18,20},{2... | collective-permute-start | bytes 393224 | tf_op jit(solution)/shard_map/ppermute | solution.py:49
  (39 other events, 206.1 us)
